TPU v7x, 512 devices: a whole 4x8x8 slice. The times are simulated.
512 devices in a mesh: gx: 8 (over y), gy: 16 (over z, core), gz: 4 (over x).
Axes of the slice: x: 4, y: 8, z: 8, core: 2. Of those that a mesh axis runs over, the one named last changes fastest.
Arguments:
- eri: bfloat16 [16384, 256, 256], P(('gx', 'gy', 'gz')), may hold values from -0.375 to 0.375
- owner: int32 [16384, 1], P(('gx', 'gy', 'gz')), may hold values from 0 to 7; in each aligned block of 32 rows (0 to 31, 32 to 63, ...) at most 8 rows name the same one
- quartet: int32 [16384, 4], P(('gx', 'gy', 'gz')), may hold values from 0 to 191, as said below
- significance: int32 [16384], P(('gx', 'gy', 'gz')), may hold values 0 or 1
- density: bfloat16 [3072, 3072], P('gy'), may hold values from -6 to 6
Outputs:
- exchange: float32 [3072, 3072], P('gx', 'gy')
Inputs may be any that keep to these rules, and one draw needn't show every extreme that they name: Among the 32 tiles of one device (aligned blocks of 32 rows), no owner value is named more than 8 times, and in some blocks one is named exactly 8 times. `quartet`: column 0 lies in 0 to 5, column 1 in 0 to 191, column 2 in 0 to 11, column 3 in 0 to 191.
All inputs are finite; a program needn't handle non-finite values. No bound on the sum of `significance` on one device may be relied on, other than what follows from the above.
Results may differ from a plain program's by a relative error of at most 0.0003.
Values sent between devices are 32-bit elements; how exact they have to be, the bound alone decides.
A program may use at most 64 MiB of HBM per device.

v0:
```python
import jax
import jax.numpy as jnp
from jax import lax
from jax.sharding import PartitionSpec as P

NBAS = 3072
SHELL = 16
TILES_DEV = 32


def place_blocks(values, row_shell, col_shell, row_count, col_count):
    slots = values.shape[0]
    row_hot = (row_shell[:, None] == jnp.arange(row_count, dtype=jnp.int32)[None, :]).astype(
        jnp.float32
    )
    col_hot = (col_shell[:, None] == jnp.arange(col_count, dtype=jnp.int32)[None, :]).astype(
        jnp.float32
    )
    spread = row_hot[:, :, None, None] * values.reshape(slots, 1, SHELL, SHELL)
    spread = spread.reshape(slots, row_count * SHELL * SHELL)
    placed = jnp.dot(
        spread.T, col_hot, precision=lax.Precision.HIGHEST, preferred_element_type=jnp.float32
    )
    placed = placed.reshape(row_count, SHELL, SHELL, col_count)
    return jnp.transpose(placed, (0, 1, 3, 2)).reshape(row_count * SHELL, col_count * SHELL)


def shards(eri, owner, quartet, significance, density):
    group_size = lax.axis_size("gx")
    shell_count = NBAS // SHELL
    slab_shells = shell_count // (group_size * lax.axis_size("gz"))
    col_shells = shell_count // lax.axis_size("gy")
    capacity = min(TILES_DEV, 2 * TILES_DEV // group_size)
    pair_size = SHELL * SHELL
    all_slots = group_size * capacity
    density_blocks = density.reshape(density.shape[0] // SHELL, SHELL, shell_count, SHELL)
    target = owner[:, 0]
    onehot = (target[:, None] == jnp.arange(group_size, dtype=jnp.int32)[None, :]).astype(jnp.int32)
    before = jnp.cumsum(onehot, axis=0) - onehot
    place_in = jnp.sum(before * onehot, axis=1)
    position = target * capacity + place_in
    placement = jnp.arange(all_slots, dtype=jnp.int32)[:, None] == position[None, :]
    blocks = density_blocks[quartet[:, 2], :, quartet[:, 3], :]
    flat_block = blocks.reshape(blocks.shape[0], pair_size)
    local_terms = jnp.einsum("tij,tj->ti", eri, flat_block, preferred_element_type=jnp.float32)
    local_terms = local_terms * significance.astype(jnp.float32)[:, None]
    result_buffer = jnp.dot(
        placement.astype(jnp.float32),
        local_terms,
        precision=lax.Precision.HIGHEST,
        preferred_element_type=jnp.float32,
    )
    index_buffer = jnp.sum(placement.astype(jnp.int32)[:, :, None] * quartet[None, :, :2], axis=1)
    summed, indices = (
        lax.all_to_all(result_buffer, "gx", split_axis=0, concat_axis=0, tiled=True),
        lax.all_to_all(index_buffer, "gx", split_axis=0, concat_axis=0, tiled=True),
    )
    every_block, every_index = (
        lax.all_gather(summed, "gy", axis=0, tiled=True),
        lax.all_gather(indices, "gy", axis=0, tiled=True),
    )
    local_ket = (every_index[:, 1] - lax.axis_index("gy") * col_shells).astype(jnp.int32)
    owned_cols = place_blocks(every_block, every_index[:, 0], local_ket, slab_shells, col_shells)
    return lax.all_gather(owned_cols, "gz", axis=0, tiled=True)


def solution(mesh):
    in_specs = (
        P(("gx", "gy", "gz"), None, None),
        P(("gx", "gy", "gz"), None),
        P(("gx", "gy", "gz"), None),
        P(("gx", "gy", "gz")),
        P("gy", None),
    )
    out_specs = P("gx", "gy")
    return jax.shard_map(shards, mesh=mesh, in_specs=in_specs, out_specs=out_specs, check_vma=False)
```

profile of v0, /device:TPU:1, one launch (start us, length us, event | category | flops | bytes accessed | tf_op | source)
XLA Modules:
  0.0 121.8 jit_solution(12481467211014356538)
XLA Ops:
  6.5 0.0 all-gather.3.cloned.1.call-start
  6.5 9.9 %reshape.74 = bf16[12,16,192,16]{3,2,1,0:T(8,128)(2,1)} reshape(bf16[192,3072]{1,0:T(8,128)(2,1)} %param.9) | data formatting | bytes 2359296 | tf_op jit(solution)/shard_map/reshape | solution.py:36
  16.4 0.0 copy-start
  16.4 0.0 copy-start.2
  16.4 0.0 copy-start.1
  16.4 0.0 slice-start
  16.4 14.7 %copy.34 = bf16[12,16,192,16]{3,1,2,0:T(8,128)(2,1)} copy(bf16[12,16,192,16]{3,2,1,0:T(8,128)(2,1)} %reshape.74) | data formatting | bytes 2359296 | tf_op jit(solution)/shard_map/reshape | solution.py:36
  31.1 0.0 copy-done
  31.1 4.3 %gather_fusion = bf16[32,16,16]{2,1,0:T(8,128)(2,1)S(1)} fusion(bf16[12,16,192,16]{3,1,2,0:T(8,128)(2,1)} %copy.34, s32[32]{0:T(128)S(1)} %fusion.22), kind=kCustom, calls=%fused_computation | custom fusion | bytes 33024 | tf_op jit(solution)/shard_map/gather | solution.py:43
  35.4 0.2 copy.35
  35.6 0.1 copy.39
  35.7 0.0 copy-done.2
  35.7 0.0 copy-done.1
  35.7 0.1 fusion.14
  35.8 0.1 reduce_window_sum.11
  35.9 0.2 select_reduce_fusion
  36.1 3.4 %fusion.23 = f32[32,1,256]{2,1,0:T(1,128)S(1)} fusion(bf16[32,256,1]{1,2,0:T(2,128)(2,1)S(1)} %copy.39, bf16[32,256,256]{2,1,0:T(8,128)(2,1)} %param.5), kind=kOutput, calls=%fused_computation.33 | convolution fusion | flops 4194304 | bytes 4243456 | tf_op jit(solution)/shard_map/tij,tj->ti/dot_general | solution.py:45
  39.4 0.3 convolution_bitcast_fusion
  39.8 14.8 %all_to_all.24 = f32[8,8,256]{2,1,0:T(8,128)} all-to-all(f32[8,8,256]{2,1,0:T(8,128)S(1)} %convolution_bitcast_fusion), channel_id=1, replica_groups=mesh['gx'=8,'gy'=16,'gz'=4] {'gx'}, dimensions={0} | all-to-all | bytes 131072 | tf_op jit(solution)/shard_map/all_to_all | solution.py:55
  54.5 0.0 all-gather.3.cloned.1.call-update
  54.5 0.1 fusion.15
  54.6 0.0 slice-done
  54.6 0.1 multiply_reduce_fusion
  54.7 0.1 all_to_all.16
  54.8 0.6 copy.31
  55.4 3.3 %all-to-all-start = ((s32[8,8,2]{1,2,0:T(2,128)}), s32[8,8,2]{1,2,0:T(2,128)S(1)}, u32[]{:S(2)}, u32[]{:S(2)}) async-start(s32[8,8,2]{1,2,0:T(2,128)} %copy.31), calls=%async_computation | async-start | bytes 16384 | tf_op jit(solution)/shard_map/all_to_all | solution.py:56
  58.8 6.5 %all-to-all-done = s32[8,8,2]{1,2,0:T(2,128)S(1)} async-done(((s32[8,8,2]{1,2,0:T(2,128)}), s32[8,8,2]{1,2,0:T(2,128)S(1)}, u32[]{:S(2)}, u32[]{:S(2)}) %all-to-all-start) | async-done | bytes 544 | tf_op jit(solution)/shard_map/all_to_all | solution.py:56
  65.3 0.1 reshape.83
  65.4 26.4 %all-gather = s32[16,64,2]{1,2,0:T(2,128)S(1)} all-gather(s32[1,64,2]{1,2,0:T(2,128)S(1)} %reshape.83), channel_id=1, replica_groups=mesh['gx'=8,'gy'=16,'gz'=4] {'gy'}, dimensions={0}, use_global_device_ids=true | all-gather | bytes 8704 | tf_op jit(solution)/shard_map/all_gather | solution.py:60
  91.8 0.1 reshape.84
  91.9 5.9 %all-gather.3.cloned.1.call-done = f32[1024,256]{1,0:T(8,128)} async-done(((f32[64,256]{1,0:T(8,128)}), f32[1024,256]{1,0:T(8,128)}) %all-gather.3.cloned.1.call-update) | async-done | bytes 1048592 | tf_op jit(solution)/shard_map/all_gather | solution.py:59
  97.8 1.6 %copy.36 = f32[1024,256]{0,1:T(8,128)S(1)} copy(f32[1024,256]{1,0:T(8,128)} %all-gather.3.cloned.1.call-done) | data formatting | bytes 2097152 | tf_op jit(solution)/shard_map/all_gather | solution.py:59
  99.4 3.1 %fusion.5 = f32[6,16,12,16]{2,3,1,0:T(8,128)S(1)} fusion(f32[1024,16,16]{0,2,1:T(8,128)S(1)} %bitcast.40, f32[1024,6]{0,1:T(8,128)S(1)} %fusion.12, s32[1024]{0:T(1024)S(1)} %bitcast.44), kind=kOutput, calls=%fused_computation.6 | convolution fusion | flops 228077568 | bytes 1150976 | tf_op jit(solution)/shard_map/dot_general | solution.py:21
  102.5 0.6 copy.37
  103.2 0.3 reshape.76
  103.4 10.7 %all_gather.11 = f32[384,192]{1,0:T(8,128)S(1)} all-gather(f32[96,192]{1,0:T(8,128)S(1)} %reshape.76), channel_id=1, replica_groups=mesh['gx'=8,'gy'=16,'gz'=4] {'gz'}, dimensions={0}, use_global_device_ids=true | all-gather | bytes 368640 | tf_op jit(solution)/shard_map/all_gather | solution.py:64
  114.1 0.9 copy.38
  (7 shorter events, 0.0 us)
Async XLA Ops:
  6.5 91.3 %all-gather.3.cloned.1.call-start = ((), (), s32[]{:S(2)}) async-start(), calls=%async_computation.2 | async-start | bytes 1114112 | tf_op jit(solution)/shard_map/all_gather | solution.py:59
  16.4 14.7 %copy-start = (s32[32,4]{0,1:T(4,128)S(1)}, s32[32,4]{0,1:T(4,128)}, u32[]{:S(2)}) copy-start(s32[32,4]{0,1:T(4,128)} %param.7) | copy-start | bytes 1540
  16.4 19.3 %copy-start.2 = (s32[32]{0:T(128)S(1)}, s32[32]{0:T(128)}, u32[]{:S(2)}) copy-start(s32[32]{0:T(128)} %param.8) | copy-start | bytes 388
  16.4 19.3 %copy-start.1 = (s32[32,1]{0,1:T(1,128)S(1)}, s32[32,1]{0,1:T(1,128)}, u32[]{:S(2)}) copy-start(s32[32,1]{0,1:T(1,128)} %param.6) | copy-start | bytes 388
  16.4 38.2 %slice-start = ((s32[32,4]{0,1:T(4,128)}), s32[32,2]{0,1:T(2,128)S(1)}, s32[]{:S(2)}) async-start(s32[32,4]{0,1:T(4,128)} %param.7), calls=%async_computation.3 | async-start | bytes 2048 | tf_op jit(solution)/shard_map/slice | solution.py:53
  55.4 9.9 %all-to-all-start = ((s32[8,8,2]{1,2,0:T(2,128)}), s32[8,8,2]{1,2,0:T(2,128)S(1)}, u32[]{:S(2)}, u32[]{:S(2)}) async-start(s32[8,8,2]{1,2,0:T(2,128)} %copy.31), calls=%async_computation | async-start | bytes 16384 | tf_op jit(solution)/shard_map/all_to_all | solution.py:56
Sparse Core Ops, SparseCore 0:
  54.7 43.1 all-gather.2
where the time goes:
time: 123 us; the launch traced here: 122 us
  blocking collectives  51.9 us (42%)
  local copies, waits for them, and re-layouts  33.4 us (27%)
  between operations  13.5 us (11%)
  waiting for transfers between devices  12.5 us (10%)
  matrix products  6.79 us (6%)
  starting transfers between devices  3.34 us (3%)
    all_gather x1, blocking collectives, shards(): lax.all_gather(indices, 'gy', axis=0, tiled=True)  26.4 us
    reshape x2, local copies, waits for them, and re-layouts, shards(): density.reshape(density.shape[0] // SHELL, SHELL, shell_count, SHELL)  24.5 us
    all_to_all x1, blocking collectives, shards(): lax.all_to_all(result_buffer, 'gx', split_axis=0, concat_axis=0, tiled=True)  14.8 us
    all_gather x1, blocking collectives, shards(): return lax.all_gather(owned_cols, 'gz', axis=0, tiled=True)  10.7 us
    all_to_all x1, waiting for transfers between devices, shards(): lax.all_to_all(index_buffer, 'gx', split_axis=0, concat_axis=0, tiled=True)  6.52 us
    all_gather x1, waiting for transfers between devices, shards(): lax.all_gather(summed, 'gy', axis=0, tiled=True)  5.92 us
    gather x2, local copies, waits for them, and re-layouts, shards(): blocks = density_blocks[quartet[:, 2], :, quartet[:, 3], :]  4.51 us
    dot_general x1, matrix products, shards(): jnp.einsum('tij,tj->ti', eri, flat_block, preferred_element_type=jnp.floa...  3.37 us
  transfers between devices with their start and end apart: 2, of which 2 were waited for; matrix products, arithmetic and copies ran while one was open for 1% of the time, Pallas kernels for 0%

commit v1 on v0

v1 whole, which is shorter than its diff:
```python
import jax
import jax.numpy as jnp
from jax import lax
from jax.experimental import pallas as pl
from jax.experimental.pallas import tpu as pltpu
from jax.sharding import PartitionSpec as P

SHELL = 16
PAIR = 256
TILES_DEV = 32
NSH = 192
N_GX = 8
N_Z = 8
N_GZ = 4
CAP = 8
ROWSH = 6
COLSH = 12
BLOCKS = ROWSH * COLSH
SLOTS = N_GX * CAP
CHUNKS = 8
MESH = pl.DeviceIdType.MESH
F32 = jnp.float32
BF16 = jnp.bfloat16
I32 = jnp.int32


def order(rel):
    return max(0, min(2 * rel - 1, 2 * (N_GX - rel)))


def iota(shape, dim):
    return lax.broadcasted_iota(I32, shape, dim)


def contract(own_s, quart_s, sig_s, dens_hbm, eri_hbm, val_ref, code_ref, dens, eri, picked, count_s, place_s, sems):
    per = TILES_DEV // CHUNKS
    dens_copy = pltpu.make_async_copy(dens_hbm, dens, sems.at[CHUNKS])
    dens_copy.start()
    copies = []
    for c in range(CHUNKS):
        part = pl.ds(c * per, per)
        copies.append(pltpu.make_async_copy(eri_hbm.at[part], eri.at[part], sems.at[c]))
        copies[-1].start()
    me = lax.axis_index("gx")
    val_ref[...] = jnp.zeros_like(val_ref)
    for i in range(N_GX):
        count_s[i] = 0
    lane = iota((1, 128), 1)
    codes = jnp.zeros((1, 128), I32)
    for t in range(TILES_DEV):
        rel = lax.rem(me - own_s[0, t] + N_GX, N_GX)
        row = jnp.maximum(0, jnp.minimum(2 * rel - 1, 2 * (N_GX - rel)))
        seen = count_s[row]
        count_s[row] = seen + 1
        place_s[t] = row * CAP + seen
        codes = jnp.where((lane & (SLOTS - 1)) == row * CAP + seen, quart_s[0, t] * NSH + quart_s[1, t], codes)
    for i in range(N_GX):
        code_ref[i] = jnp.where(((lane & (SLOTS - 1)) >> 3) == i, codes, 0)
    dens_copy.wait()
    group = iota((SHELL, 128), 1) >> 4
    for t in range(TILES_DEV):
        shell = quart_s[3, t]
        start = pl.multiple_of(quart_s[2, t] * SHELL, SHELL)
        column = pl.multiple_of((shell >> 3) * 128, 128)
        block = dens[pl.ds(start, SHELL), pl.ds(column, 128)].astype(F32)
        wanted = jnp.where(sig_s[0, t] != 0, shell & 7, -1)
        picked[t * SHELL:(t + 1) * SHELL, :] = jnp.where(group == wanted, block, 0.0)
    fold = ((iota((128, PAIR), 0) & 15) == (iota((128, PAIR), 1) & 15)).astype(F32).astype(BF16)
    wide = jnp.dot(picked[...].astype(BF16), fold, preferred_element_type=F32)
    rows = TILES_DEV * SHELL
    wide = jnp.where((iota((rows, PAIR), 0) & 15) == (iota((rows, PAIR), 1) >> 4), wide, 0.0).astype(BF16)
    gather = (iota((128, rows), 0) == (iota((128, rows), 1) >> 4)).astype(F32).astype(BF16)
    flat = jnp.dot(gather, wide, preferred_element_type=F32)
    weights = flat.T.astype(BF16)
    acc = jnp.zeros((PAIR, 128), F32)
    lanes = iota((PAIR, 128), 1)
    for c in range(CHUNKS):
        copies[c].wait()
        for t in range(c * per, (c + 1) * per):
            term = jnp.dot(eri[t], weights, preferred_element_type=F32)
            acc = jnp.where(lanes == t, term, acc)
    terms = acc.T
    for t in range(TILES_DEV):
        val_ref[pl.ds(place_s[t], 1), :] = terms[t:t + 1, :]


def exchange(val_ref, code_ref, out_ref, held, ycode, zcode, mine, half, arrived,
             ysend, yrecv, ycsend, ycrecv, zcsend, zcrecv, rsend, rrecv, psend, precv, xsend, xrecv):
    gx, gy, gz = lax.axis_index("gx"), lax.axis_index("gy"), lax.axis_index("gz")
    z, core = gy // 2, lax.rem(gy, 2)

    def along_x(d):
        return {"gx": lax.rem(gx + N_GX - d, N_GX)}

    def along_z(d):
        return {"gy": lax.rem(z + d + N_Z, N_Z) * 2 + core}

    def along_gz(d):
        return {"gz": lax.rem(gz + d, N_GZ)}

    partner = {"gy": z * 2 + 1 - core}
    barrier = pltpu.get_barrier_semaphore()
    peers = [along_x(d) for d in range(1, N_GX)] + [along_z(d) for d in range(1, N_Z)]
    peers += [along_gz(d) for d in range(1, N_GZ)] + [partner]
    for peer in peers:
        pl.semaphore_signal(barrier, inc=1, device_id=peer, device_id_type=MESH)
    pl.semaphore_wait(barrier, len(peers))

    def send(src, dst, s, r, peer):
        copy = pltpu.make_async_remote_copy(src_ref=src, dst_ref=dst, send_sem=s, recv_sem=r, device_id=peer, device_id_type=MESH)
        copy.start()
        return copy

    started = []
    near = [1, 7, 2]
    far = [6, 3, 5, 4]
    code_in, val_in = {}, {}
    for d in near + far:
        r = order(d)
        code_in[d] = send(code_ref.at[r], ycode.at[r], ycsend.at[r], ycrecv.at[r], along_x(d))
    for d in far[::-1] + near[::-1]:
        r = order(d)
        val_in[d] = send(val_ref.at[pl.ds(r * CAP, CAP)], held.at[0, pl.ds(r * CAP, CAP)], ysend.at[r], yrecv.at[r], along_x(d))
    held[0, 0:CAP, :] = val_ref[0:CAP, :]
    for d in near + far:
        code_in[d].wait_recv()
    total = code_ref[0]
    for r in range(1, N_GX):
        total = total + ycode[r]
    mine[...] = total
    zcode[0] = total
    zcode_in = []
    for d, slot in ((1, 1), (7, 2), (2, 3), (6, 4), (3, 5), (5, 6), (4, 7)):
        zcode_in.append(send(mine, zcode.at[slot], zcsend.at[slot], zcrecv.at[slot], along_z(d)))

    GR = SLOTS // 2

    def hop(src, direction, dst, g):
        part = pl.ds(g * GR, GR)
        i = (dst * 2 + g) if dst < 7 else (14 + g)
        c = send(held.at[src, part], held.at[dst, part], rsend.at[i], rrecv.at[i], along_z(direction))
        started.append(c)
        return c

    inward = {}
    for g, ds in ((0, near), (1, far)):
        for d in ds:
            val_in[d].wait_recv()
        inward[1, g] = hop(0, 1, 1, g)
        inward[2, g] = hop(0, -1, 2, g)

    rows = iota((2 * BLOCKS, 128), 0)
    other = (rows >= BLOCKS).astype(I32)
    inner = rows - other * BLOCKS
    bra = jnp.zeros_like(inner)
    for i in range(1, ROWSH):
        bra = bra + (inner >= i * COLSH).astype(I32)
    ket = inner - bra * COLSH
    column = jnp.where(other == 1, (z * 2 + 1 - core) * COLSH, gy * COLSH)
    wanted = bra * NSH + column + ket
    lane = iota((1, 128), 1)

    def place(a, b, acc):
        code = jnp.where(lane < SLOTS, zcode[a], zcode[b])
        hot = (wanted == code).astype(F32).astype(BF16)
        hot = jnp.concatenate([hot, hot], axis=1)
        values = jnp.concatenate([held[a], held[b]], axis=0)
        top = values.astype(BF16)
        low = (values - top.astype(F32)).astype(BF16)
        return acc + jnp.dot(hot, jnp.concatenate([top, low], axis=0), preferred_element_type=F32)

    acc = jnp.zeros((2 * BLOCKS, PAIR), F32)
    for c in zcode_in:
        c.wait_recv()
    for h in (1, 2, 3):
        left, right = 2 * h - 1, 2 * h
        for g in (0, 1):
            inward[left, g].wait_recv()
            if h < 3:
                inward[left + 2, g] = hop(left, 1, left + 2, g)
            elif g == 0:
                inward[7, 0] = hop(left, 1, 7, 0)
            inward[right, g].wait_recv()
            if h < 3:
                inward[right + 2, g] = hop(right, -1, right + 2, g)
            elif g == 1:
                inward[7, 1] = hop(right, -1, 7, 1)
        acc = place(left, right, acc)
    inward[7, 0].wait_recv()
    inward[7, 1].wait_recv()
    acc = place(0, 7, acc)
    half[...] = acc[BLOCKS:]
    give = send(half, arrived, psend, precv, partner)
    give.wait_recv()
    final = acc[:BLOCKS] + arrived[...]
    out_ref[0, gz] = final[:, :128]
    out_ref[1, gz] = final[:, 128:]
    last = []
    for d in range(1, N_GZ):
        last.append(send(out_ref.at[:, gz], out_ref.at[:, gz], xsend.at[d - 1], xrecv.at[d - 1], along_gz(d)))
    for c in last:
        c.wait_recv()
    for c in list(code_in.values()) + list(val_in.values()) + zcode_in + started + [give] + last:
        c.wait_send()


def assemble(got_ref, out_ref, wide):
    group = iota((4 * ROWSH, 128), 1) >> 4
    pieces = [[got_ref[pl.ds(h * N_GZ * BLOCKS + k, 4 * ROWSH, stride=COLSH), :] for h in range(2)] for k in range(COLSH)]
    for a in range(SHELL):
        for j, ks in enumerate((range(8), range(8, COLSH))):
            line = jnp.zeros((4 * ROWSH, 128), F32)
            for k in ks:
                shift = ((k - a) % 8) * 16
                src = pieces[k][a // 8]
                moved = pltpu.roll(src, shift, 1) if shift else src
                line = jnp.where(group == k % 8, moved, line)
            wide[j, pl.ds(a, 4 * ROWSH, stride=SHELL), :] = line
    out_ref[:128, :] = wide[0].T
    out_ref[128:, :] = wide[1].T[:NSH - 128, :]


def shards(eri, owner, quartet, significance, density):
    any_spec = pl.BlockSpec(memory_space=pl.ANY)
    smem = pl.BlockSpec(memory_space=pltpu.SMEM)
    vmem = pl.BlockSpec(memory_space=pltpu.VMEM)
    values, codes = pl.pallas_call(
        contract,
        out_shape=(jax.ShapeDtypeStruct((SLOTS, PAIR), F32), jax.ShapeDtypeStruct((N_GX, 1, 128), I32)),
        in_specs=[smem, smem, smem, any_spec, any_spec],
        out_specs=(vmem, vmem),
        scratch_shapes=[
            pltpu.VMEM(density.shape, BF16),
            pltpu.VMEM(eri.shape, BF16),
            pltpu.VMEM((TILES_DEV * SHELL, 128), F32),
            pltpu.SMEM((N_GX,), I32),
            pltpu.SMEM((TILES_DEV,), I32),
            pltpu.SemaphoreType.DMA((CHUNKS + 1,)),
        ],
        name="contract",
    )(owner.T, quartet.T, significance[None, :], density, eri)
    dma = pltpu.SemaphoreType.DMA
    got = pl.pallas_call(
        exchange,
        out_shape=jax.ShapeDtypeStruct((2, N_GZ, BLOCKS, 128), F32),
        in_specs=[vmem, vmem],
        out_specs=vmem,
        scratch_shapes=[
            pltpu.VMEM((N_Z, SLOTS, PAIR), F32),
            pltpu.VMEM((N_GX, 1, 128), I32),
            pltpu.VMEM((N_Z, 1, 128), I32),
            pltpu.VMEM((1, 128), I32),
            pltpu.VMEM((BLOCKS, PAIR), F32),
            pltpu.VMEM((BLOCKS, PAIR), F32),
            dma((N_GX,)), dma((N_GX,)), dma((N_GX,)), dma((N_GX,)), dma((N_Z,)), dma((N_Z,)),
            dma((16,)), dma((16,)), dma, dma, dma((N_GZ,)), dma((N_GZ,)),
        ],
        compiler_params=pltpu.CompilerParams(collective_id=0, has_side_effects=True),
        name="exchange",
    )(values, codes)
    turned = pl.pallas_call(
        assemble,
        out_shape=jax.ShapeDtypeStruct((NSH, N_GZ * ROWSH * SHELL), F32),
        in_specs=[vmem],
        out_specs=vmem,
        scratch_shapes=[pltpu.VMEM((2, N_GZ * ROWSH * SHELL, 128), F32)],
        name="assemble",
    )(got.reshape(2 * N_GZ * BLOCKS, 128))
    return turned.T


def solution(mesh):
    in_specs = (
        P(("gx", "gy", "gz"), None, None),
        P(("gx", "gy", "gz"), None),
        P(("gx", "gy", "gz"), None),
        P(("gx", "gy", "gz")),
        P("gy", None),
    )
    return jax.shard_map(shards, mesh=mesh, in_specs=in_specs, out_specs=P("gx", "gy"), check_vma=False)
```

time: 123 us -> 52.2 us (0.42)
  Pallas kernels: 0 us -> 52 us
  blocking collectives: 51.9 us -> 0 us
  local copies, waits for them, and re-layouts: 33.4 us -> 0 us
  between operations: 13.5 us -> 0.02 us
  waiting for transfers between devices: 12.5 us -> 0 us
  matrix products: 6.79 us -> 0 us
  starting transfers between devices: 3.34 us -> 0 us
    pallas_call x0 -> x3, Pallas kernels: none -> 52 us  [the longest x1 44.1 us: shards(): pl.pallas_call(exchange, out_shape=jax.ShapeDtypeStruct((2, N_GZ, BLOCKS,...]
    all_gather x2 -> x0, blocking collectives: 37.1 us -> none  [the longest x1 26.4 us: shards(): lax.all_gather(indices, 'gy', axis=0, tiled=True)]
    reshape x4 -> x0, local copies, waits for them, and re-layouts: 24.9 us -> none  [the longest x2 24.5 us: shards(): density.reshape(density.shape[0] // SHELL, SHELL, shell_count, SHELL)]
    all_to_all x1 -> x0, blocking collectives: 14.8 us -> none  [shards(): lax.all_to_all(result_buffer, 'gx', split_axis=0, concat_axis=0, tiled=True)]
    dot_general x3 -> x0, matrix products: 6.79 us -> none  [the longest x1 3.37 us: shards(): jnp.einsum('tij,tj->ti', eri, flat_block, preferred_element_type=jnp.floa...]
    all_to_all x1 -> x0, waiting for transfers between devices: 6.52 us -> none  [shards(): lax.all_to_all(index_buffer, 'gx', split_axis=0, concat_axis=0, tiled=True)]
    all_gather x1 -> x0, waiting for transfers between devices: 5.92 us -> none  [shards(): lax.all_gather(summed, 'gy', axis=0, tiled=True)]
    gather x2 -> x0, local copies, waits for them, and re-layouts: 4.51 us -> none  [shards(): blocks = density_blocks[quartet[:, 2], :, quartet[:, 3], :]]
  transfers between devices with their start and end apart: 2 -> 0, of which waited for: 2 -> 0; matrix products, arithmetic and copies ran while one was open for 1% -> 0% of each run, Pallas kernels for 0% -> 0%
where the time goes in v1:
time: 52.2 us; the launch traced here: 52 us
  Pallas kernels  52 us (100%)
    pallas_call x1, Pallas kernels, shards(): pl.pallas_call(exchange, out_shape=jax.ShapeDtypeStruct((2, N_GZ, BLOCKS,...  44.1 us
    pallas_call x1, Pallas kernels, shards(): pl.pallas_call(contract, out_shape=(jax.ShapeDtypeStruct((SLOTS, PAIR), F...  5.47 us
    pallas_call x1, Pallas kernels, shards(): pl.pallas_call(assemble, out_shape=jax.ShapeDtypeStruct((NSH, N_GZ * ROWS...  2.44 us

profile of v1, /device:TPU:1, one launch (start us, length us, event | category | flops | bytes accessed | tf_op | source)
XLA Modules:
  0.0 52.0 jit_solution(18040573728027610188)
XLA Ops:
  0.0 5.5 %contract.1 = (f32[64,256]{1,0:T(8,128)}, s32[8,1,128]{2,1,0:T(1,128)}) custom-call(s32[1,32]{1,0:T(1,128)} %bitcast.7, s32[4,32]{1,0:T(4,128)} %bitcast.6, s32[1,32]{1,0:T(1,128)} %bitcast.8, bf16[192,3072]{1,0:T(8,128)(2,1)} %dens_hbm.1, bf16[32,256,256]{2,1,0:T(8,128)(2,1)} %eri_hbm.1), custom_call_target="tpu_custom_call" | custom-call | tf_op jit(solution)/shard_map/contract/pallas_call | solution.py:227
  5.5 44.1 %exchange.1 = f32[2,4,72,128]{3,2,1,0:T(8,128)} custom-call(f32[64,256]{1,0:T(8,128)} %get-tuple-element.7.val_ref, s32[8,1,128]{2,1,0:T(1,128)} %get-tuple-element.8.code_ref), custom_call_target="tpu_custom_call" | custom-call | tf_op jit(solution)/shard_map/exchange/pallas_call | solution.py:243
  49.5 2.4 %assemble.1 = f32[192,384]{1,0:T(8,128)} custom-call(f32[576,128]{1,0:T(8,128)} %bitcast.5), custom_call_target="tpu_custom_call" | custom-call | tf_op jit(solution)/shard_map/assemble/pallas_call | solution.py:261

commit v2 on v1

v2 whole, which is shorter than its diff:
```python
import jax
import jax.numpy as jnp
from jax import lax
from jax.experimental import pallas as pl
from jax.experimental.pallas import tpu as pltpu
from jax.sharding import PartitionSpec as P

SHELL = 16
PAIR = 256
TILES_DEV = 32
NSH = 192
N_GX = 8
N_Z = 8
N_GZ = 4
CAP = 8
ROWSH = 6
COLSH = 12
BLOCKS = ROWSH * COLSH
SLOTS = N_GX * CAP
CHUNKS = 8
DCHUNKS = 24
MESH = pl.DeviceIdType.MESH
F32 = jnp.float32
BF16 = jnp.bfloat16
I32 = jnp.int32


def order(rel):
    return max(0, min(2 * rel - 1, 2 * (N_GX - rel)))


def iota(shape, dim):
    return lax.broadcasted_iota(I32, shape, dim)


def fused(own_s, quart_s, sig_s, dens_hbm, eri_hbm, out_ref, dens, eri, picked, vals, codes_out, held, ycode, zcode, mine, hots, half, arrived,
          dsem, esem, ysend, yrecv, ycsend, ycrecv, zcsend, zcrecv, rsend, rrecv, psend, precv, xsend, xrecv):
    gx, gy, gz = lax.axis_index("gx"), lax.axis_index("gy"), lax.axis_index("gz")
    z, core = gy // 2, lax.rem(gy, 2)

    def along_x(d):
        return {"gx": lax.rem(gx + N_GX - d, N_GX)}

    def along_z(d):
        return {"gy": lax.rem(z + d + N_Z, N_Z) * 2 + core}

    def along_gz(d):
        return {"gz": lax.rem(gz + d + N_GZ, N_GZ)}

    partner = {"gy": z * 2 + 1 - core}
    loads = []
    for c in range(DCHUNKS):
        loads.append(pltpu.make_async_copy(dens_hbm.at[:, :, pl.ds(c * 128, 128)], dens.at[pl.ds(c * COLSH, COLSH)], dsem.at[c]))
        loads[-1].start()
    per = TILES_DEV // CHUNKS
    copies = []
    for c in range(CHUNKS):
        part = pl.ds(c * per, per)
        copies.append(pltpu.make_async_copy(eri_hbm.at[part], eri.at[part], esem.at[c]))
        copies[-1].start()
    barrier = pltpu.get_barrier_semaphore()
    peers = [along_x(d) for d in range(1, N_GX)] + [along_z(d) for d in range(1, N_Z)]
    peers += [along_gz(1), along_gz(-1), partner]
    for peer in peers:
        pl.semaphore_signal(barrier, inc=1, device_id=peer, device_id_type=MESH)

    rows = TILES_DEV * SHELL
    lane = iota((1, 128), 1)
    tile = iota((1, rows), 1) >> 4
    codes = jnp.zeros((1, 128), I32)
    spread = jnp.zeros((1, rows), I32)
    counts = jnp.int32(0)
    places = []
    for t in range(TILES_DEV):
        rel = (gx - own_s[0, t] + N_GX) & (N_GX - 1)
        row = jnp.maximum(0, jnp.minimum(2 * rel - 1, 2 * (N_GX - rel)))
        seen = (counts >> (row * 4)) & 15
        counts = counts + (jnp.int32(1) << (row * 4))
        slot = row * CAP + seen
        places.append(slot)
        codes = jnp.where((lane & (SLOTS - 1)) == slot, quart_s[0, t] * NSH + quart_s[1, t], codes)
        spread = jnp.where(tile == t, slot, spread)
    for i in range(N_GX):
        codes_out[i] = jnp.where(((lane & (SLOTS - 1)) >> 3) == i, codes, 0)
    gather = (iota((128, rows), 0) == spread).astype(F32).astype(BF16)
    fold = ((iota((128, PAIR), 0) & 15) == (iota((128, PAIR), 1) & 15)).astype(F32).astype(BF16)
    for load in loads:
        load.wait()
    group = iota((SHELL, 128), 1) >> 4
    for t in range(TILES_DEV):
        shell = quart_s[3, t]
        block = dens[(shell >> 3) * COLSH + quart_s[2, t]].astype(F32)
        wanted = jnp.where(sig_s[0, t] != 0, shell & 7, -1)
        picked[t * SHELL:(t + 1) * SHELL, :] = jnp.where(group == wanted, block, 0.0)
    wide = jnp.dot(picked[...].astype(BF16), fold, preferred_element_type=F32)
    wide = jnp.where((iota((rows, PAIR), 0) & 15) == (iota((rows, PAIR), 1) >> 4), wide, 0.0).astype(BF16)
    flat = jnp.dot(gather, wide, preferred_element_type=F32)
    weights = flat.T.astype(BF16)
    terms = jnp.zeros((PAIR, 128), F32)
    lanes = iota((PAIR, 128), 1)
    for c in range(CHUNKS):
        copies[c].wait()
        for t in range(c * per, (c + 1) * per):
            term = jnp.dot(eri[t], weights, preferred_element_type=F32)
            terms = jnp.where(lanes == places[t], term, terms)
    turned = terms.T
    vals[...] = turned[:SLOTS]
    held[0, 0:CAP, :] = turned[:CAP]

    pl.semaphore_wait(barrier, len(peers))

    def send(src, dst, s, r, peer):
        copy = pltpu.make_async_remote_copy(src_ref=src, dst_ref=dst, send_sem=s, recv_sem=r, device_id=peer, device_id_type=MESH)
        copy.start()
        return copy

    near = [1, 7, 2]
    far = [6, 3, 5, 4]
    code_in, val_in = {}, {}
    for d in far[::-1] + near[::-1]:
        r = order(d)
        code_in[d] = send(codes_out.at[r], ycode.at[r], ycsend.at[r], ycrecv.at[r], along_x(d))
        val_in[d] = send(vals.at[pl.ds(r * CAP, CAP)], held.at[0, pl.ds(r * CAP, CAP)], ysend.at[r], yrecv.at[r], along_x(d))

    started = []
    GR = SLOTS // 2

    def hop(src, distance, dst, g):
        part = pl.ds(g * GR, GR)
        i = dst * 2 + g
        c = send(held.at[src, part], held.at[dst, part], rsend.at[i], rrecv.at[i], along_z(distance))
        started.append(c)
        inward[dst, g] = c

    inward = {}
    rows = iota((2 * BLOCKS, 128), 0)
    other = (rows >= BLOCKS).astype(I32)
    inner = rows - other * BLOCKS
    bra = jnp.zeros_like(inner)
    for i in range(1, ROWSH):
        bra = bra + (inner >= i * COLSH).astype(I32)
    ket = inner - bra * COLSH
    column = jnp.where(other == 1, (z * 2 + 1 - core) * COLSH, gy * COLSH)
    wanted = bra * NSH + column + ket

    for g, ds in ((0, near), (1, far)):
        for d in ds:
            val_in[d].wait_recv()
        hop(0, 2, 3, g)
        hop(0, -2, 4, g)
        hop(0, 1, 1, g)
        hop(0, -1, 2, g)
    for d in near + far:
        code_in[d].wait_recv()
    total = codes_out[0]
    for r in range(1, N_GX):
        total = total + ycode[r]
    mine[...] = total
    zcode[0] = total
    zcode_in = []
    for d, slot in ((4, 7), (3, 5), (5, 6), (2, 3), (6, 4), (1, 1), (7, 2)):
        zcode_in.append(send(mine, zcode.at[slot], zcsend.at[slot], zcrecv.at[slot], along_z(d)))

    inward[3, 0].wait_recv()
    hop(3, 2, 7, 0)
    hop(3, 1, 5, 0)
    inward[4, 0].wait_recv()
    hop(4, -1, 6, 0)
    inward[4, 1].wait_recv()
    hop(4, -2, 7, 1)
    hop(4, -1, 6, 1)
    inward[3, 1].wait_recv()
    hop(3, 1, 5, 1)

    for c in zcode_in:
        c.wait_recv()
    pairs = [(1, 2), (3, 4), (5, 6), (0, 7)]
    for i, (a, b) in enumerate(pairs):
        code = jnp.where(lane < SLOTS, zcode[a], zcode[b])
        hot = (wanted == code).astype(F32).astype(BF16)
        hots[i, :, 0:128] = hot
        hots[i, :, 128:256] = hot

    acc = jnp.zeros((2 * BLOCKS, PAIR), F32)
    for i, (a, b) in enumerate(pairs):
        for s in (a, b):
            if s not in (0, 3, 4):
                inward[s, 0].wait_recv()
                inward[s, 1].wait_recv()
        values = jnp.concatenate([held[a], held[b]], axis=0)
        top = values.astype(BF16)
        low = (values - top.astype(F32)).astype(BF16)
        acc = acc + jnp.dot(hots[i], jnp.concatenate([top, low], axis=0), preferred_element_type=F32)
    half[...] = acc[BLOCKS:]
    give = send(half, arrived, psend, precv, partner)
    give.wait_recv()
    final = acc[:BLOCKS] + arrived[...]
    out_ref[0, gz] = final[:, :128]
    out_ref[1, gz] = final[:, 128:]

    def pass_on(h, owner, i, direction):
        part = out_ref.at[h, owner]
        c = send(part, part, xsend.at[i], xrecv.at[i], along_gz(direction))
        started.append(c)
        return c

    prev, nxt = lax.rem(gz + N_GZ - 1, N_GZ), lax.rem(gz + 1, N_GZ)
    up0 = pass_on(0, gz, 0, 1)
    down1 = pass_on(1, gz, 1, -1)
    up1 = pass_on(1, gz, 2, 1)
    down0 = pass_on(0, gz, 3, -1)
    up0.wait_recv()
    two0 = pass_on(0, prev, 4, 1)
    down1.wait_recv()
    two1 = pass_on(1, nxt, 5, -1)
    for c in (up1, down0, two0, two1):
        c.wait_recv()
    for c in list(code_in.values()) + list(val_in.values()) + zcode_in + started + [give]:
        c.wait_send()


def assemble(got_ref, out_ref, wide):
    group = iota((4 * ROWSH, 128), 1) >> 4
    pieces = [[got_ref[pl.ds(h * N_GZ * BLOCKS + k, 4 * ROWSH, stride=COLSH), :] for h in range(2)] for k in range(COLSH)]
    for a in range(SHELL):
        for j, ks in enumerate((range(8), range(8, COLSH))):
            line = jnp.zeros((4 * ROWSH, 128), F32)
            for k in ks:
                shift = ((k - a) % 8) * 16
                src = pieces[k][a // 8]
                moved = pltpu.roll(src, shift, 1) if shift else src
                line = jnp.where(group == k % 8, moved, line)
            wide[j, pl.ds(a, 4 * ROWSH, stride=SHELL), :] = line
    out_ref[:128, :] = wide[0].T
    out_ref[128:, :] = wide[1].T[:NSH - 128, :]


def shards(eri, owner, quartet, significance, density):
    hbm = pl.BlockSpec(memory_space=pltpu.HBM)
    smem = pl.BlockSpec(memory_space=pltpu.SMEM)
    vmem = pl.BlockSpec(memory_space=pltpu.VMEM)
    dma = pltpu.SemaphoreType.DMA
    got = pl.pallas_call(
        fused,
        out_shape=jax.ShapeDtypeStruct((2, N_GZ, BLOCKS, 128), F32),
        in_specs=[smem, smem, smem, hbm, hbm],
        out_specs=vmem,
        scratch_shapes=[
            pltpu.VMEM((DCHUNKS * COLSH, SHELL, 128), BF16),
            pltpu.VMEM(eri.shape, BF16),
            pltpu.VMEM((TILES_DEV * SHELL, 128), F32),
            pltpu.VMEM((SLOTS, PAIR), F32),
            pltpu.VMEM((N_GX, 1, 128), I32),
            pltpu.VMEM((N_Z, SLOTS, PAIR), F32),
            pltpu.VMEM((N_GX, 1, 128), I32),
            pltpu.VMEM((N_Z, 1, 128), I32),
            pltpu.VMEM((1, 128), I32),
            pltpu.VMEM((4, 2 * BLOCKS, PAIR), BF16),
            pltpu.VMEM((BLOCKS, PAIR), F32),
            pltpu.VMEM((BLOCKS, PAIR), F32),
            dma((DCHUNKS,)), dma((CHUNKS,)),
            dma((N_GX,)), dma((N_GX,)), dma((N_GX,)), dma((N_GX,)), dma((N_Z,)), dma((N_Z,)),
            dma((16,)), dma((16,)), dma, dma, dma((6,)), dma((6,)),
        ],
        compiler_params=pltpu.CompilerParams(collective_id=0, has_side_effects=True, vmem_limit_bytes=66600000),
        name="fused",
    )(owner.T, quartet.T, significance[None, :], density.reshape(COLSH, SHELL, density.shape[1]), eri)
    turned = pl.pallas_call(
        assemble,
        out_shape=jax.ShapeDtypeStruct((NSH, N_GZ * ROWSH * SHELL), F32),
        in_specs=[vmem],
        out_specs=vmem,
        scratch_shapes=[pltpu.VMEM((2, N_GZ * ROWSH * SHELL, 128), F32)],
        compiler_params=pltpu.CompilerParams(vmem_limit_bytes=66600000),
        name="assemble",
    )(got.reshape(2 * N_GZ * BLOCKS, 128))
    return turned.T


def solution(mesh):
    in_specs = (
        P(("gx", "gy", "gz"), None, None),
        P(("gx", "gy", "gz"), None),
        P(("gx", "gy", "gz"), None),
        P(("gx", "gy", "gz")),
        P("gy", None),
    )
    return jax.shard_map(shards, mesh=mesh, in_specs=in_specs, out_specs=P("gx", "gy"), check_vma=False)
```

time: 52.2 us -> 42.4 us (0.81)
  Pallas kernels: 52 us -> 42.3 us
    pallas_call x2 -> x1, Pallas kernels: 49.5 us -> 39.8 us  [shards(): pl.pallas_call(fused, out_shape=jax.ShapeDtypeStruct((2, N_GZ, BLOCKS, 12...]
where the time goes in v2:
time: 42.4 us; the launch traced here: 42.3 us
  Pallas kernels  42.3 us (100%)
    pallas_call x1, Pallas kernels, shards(): pl.pallas_call(fused, out_shape=jax.ShapeDtypeStruct((2, N_GZ, BLOCKS, 12...  39.8 us
    pallas_call x1, Pallas kernels, shards(): pl.pallas_call(assemble, out_shape=jax.ShapeDtypeStruct((NSH, N_GZ * ROWS...  2.44 us

profile of v2, /device:TPU:1, one launch (start us, length us, event | category | flops | bytes accessed | tf_op | source)
XLA Modules:
  0.0 42.3 jit_solution(6356879750114402272)
XLA Ops:
  0.0 39.8 %fused.1 = f32[2,4,72,128]{3,2,1,0:T(8,128)} custom-call(s32[1,32]{1,0:T(1,128)} %bitcast.9, s32[4,32]{1,0:T(4,128)} %bitcast.8, s32[1,32]{1,0:T(1,128)} %bitcast.10, bf16[12,16,3072]{2,1,0:T(8,128)(2,1)} %bitcast.7, bf16[32,256,256]{2,1,0:T(8,128)(2,1)} %eri_hbm.1), custom_call_target="tpu_custom_call" | custom-call | tf_op jit(solution)/shard_map/fused/pallas_call | solution.py:243
  39.8 2.4 %assemble.1 = f32[192,384]{1,0:T(8,128)} custom-call(f32[576,128]{1,0:T(8,128)} %bitcast.6), custom_call_target="tpu_custom_call" | custom-call | tf_op jit(solution)/shard_map/assemble/pallas_call | solution.py:268

commit v3 on v2

--- a/solution.py
+++ b/solution.py
@@ -33,7 +33,7 @@
     return lax.broadcasted_iota(I32, shape, dim)
 
 
-def fused(own_s, quart_s, sig_s, dens_hbm, eri_hbm, out_ref, dens, eri, picked, vals, codes_out, held, ycode, zcode, mine, hots, half, arrived,
+def fused(own_h, quart_h, sig_h, dens_hbm, eri_hbm, out_ref, own_s, quart_s, sig_s, isem, dens, eri, picked, vals, codes_out, held, ycode, zcode, mine, hots, half, arrived,
           dsem, esem, ysend, yrecv, ycsend, ycrecv, zcsend, zcrecv, rsend, rrecv, psend, precv, xsend, xrecv):
     gx, gy, gz = lax.axis_index("gx"), lax.axis_index("gy"), lax.axis_index("gz")
     z, core = gy // 2, lax.rem(gy, 2)
@@ -48,6 +48,10 @@
         return {"gz": lax.rem(gz + d + N_GZ, N_GZ)}
 
     partner = {"gy": z * 2 + 1 - core}
+    ints = []
+    for i, (src, dst) in enumerate(((own_h, own_s), (quart_h, quart_s), (sig_h, sig_s))):
+        ints.append(pltpu.make_async_copy(src, dst, isem.at[i]))
+        ints[-1].start()
     loads = []
     for c in range(DCHUNKS):
         loads.append(pltpu.make_async_copy(dens_hbm.at[:, :, pl.ds(c * 128, 128)], dens.at[pl.ds(c * COLSH, COLSH)], dsem.at[c]))
@@ -71,6 +75,8 @@
     spread = jnp.zeros((1, rows), I32)
     counts = jnp.int32(0)
     places = []
+    for c in ints:
+        c.wait()
     for t in range(TILES_DEV):
         rel = (gx - own_s[0, t] + N_GX) & (N_GX - 1)
         row = jnp.maximum(0, jnp.minimum(2 * rel - 1, 2 * (N_GX - rel)))
@@ -95,17 +101,18 @@
     wide = jnp.dot(picked[...].astype(BF16), fold, preferred_element_type=F32)
     wide = jnp.where((iota((rows, PAIR), 0) & 15) == (iota((rows, PAIR), 1) >> 4), wide, 0.0).astype(BF16)
     flat = jnp.dot(gather, wide, preferred_element_type=F32)
-    weights = flat.T.astype(BF16)
-    terms = jnp.zeros((PAIR, 128), F32)
-    lanes = iota((PAIR, 128), 1)
-    for c in range(CHUNKS):
-        copies[c].wait()
-        for t in range(c * per, (c + 1) * per):
-            term = jnp.dot(eri[t], weights, preferred_element_type=F32)
-            terms = jnp.where(lanes == places[t], term, terms)
-    turned = terms.T
-    vals[...] = turned[:SLOTS]
-    held[0, 0:CAP, :] = turned[:CAP]
+    weights = flat[:SLOTS].astype(BF16)
+    terms = jnp.zeros((SLOTS, PAIR), F32)
+    slots = iota((SLOTS, PAIR), 0)
+    for c in copies:
+        c.wait()
+    step = 4
+    for t in range(0, TILES_DEV, step):
+        many = lax.dot_general(weights, eri[t:t + step].reshape(step * PAIR, PAIR), (((1,), (1,)), ((), ())), preferred_element_type=F32)
+        for i in range(step):
+            terms = jnp.where(slots == places[t + i], many[:, i * PAIR:(i + 1) * PAIR], terms)
+    vals[...] = terms
+    held[0, 0:CAP, :] = terms[:CAP]
 
     pl.semaphore_wait(barrier, len(peers))
 
@@ -237,15 +244,19 @@
 
 def shards(eri, owner, quartet, significance, density):
     hbm = pl.BlockSpec(memory_space=pltpu.HBM)
-    smem = pl.BlockSpec(memory_space=pltpu.SMEM)
     vmem = pl.BlockSpec(memory_space=pltpu.VMEM)
     dma = pltpu.SemaphoreType.DMA
+    operands = (owner.T, quartet.T, significance[None, :], density.reshape(COLSH, SHELL, density.shape[1]), eri)
     got = pl.pallas_call(
         fused,
         out_shape=jax.ShapeDtypeStruct((2, N_GZ, BLOCKS, 128), F32),
-        in_specs=[smem, smem, smem, hbm, hbm],
+        in_specs=[hbm] * 5,
         out_specs=vmem,
         scratch_shapes=[
+            pltpu.SMEM((1, TILES_DEV), I32),
+            pltpu.SMEM((4, TILES_DEV), I32),
+            pltpu.SMEM((1, TILES_DEV), I32),
+            dma((3,)),
             pltpu.VMEM((DCHUNKS * COLSH, SHELL, 128), BF16),
             pltpu.VMEM(eri.shape, BF16),
             pltpu.VMEM((TILES_DEV * SHELL, 128), F32),
@@ -262,16 +273,16 @@
             dma((N_GX,)), dma((N_GX,)), dma((N_GX,)), dma((N_GX,)), dma((N_Z,)), dma((N_Z,)),
             dma((16,)), dma((16,)), dma, dma, dma((6,)), dma((6,)),
         ],
-        compiler_params=pltpu.CompilerParams(collective_id=0, has_side_effects=True, vmem_limit_bytes=66600000),
+        compiler_params=pltpu.CompilerParams(collective_id=0, has_side_effects=True, vmem_limit_bytes=16000000),
         name="fused",
-    )(owner.T, quartet.T, significance[None, :], density.reshape(COLSH, SHELL, density.shape[1]), eri)
+    )(*[pltpu.with_memory_space_constraint(a, pltpu.HBM) for a in operands])
     turned = pl.pallas_call(
         assemble,
         out_shape=jax.ShapeDtypeStruct((NSH, N_GZ * ROWSH * SHELL), F32),
         in_specs=[vmem],
         out_specs=vmem,
         scratch_shapes=[pltpu.VMEM((2, N_GZ * ROWSH * SHELL, 128), F32)],
-        compiler_params=pltpu.CompilerParams(vmem_limit_bytes=66600000),
+        compiler_params=pltpu.CompilerParams(vmem_limit_bytes=16000000),
         name="assemble",
     )(got.reshape(2 * N_GZ * BLOCKS, 128))
     return turned.T

time: 42.4 us -> 39.1 us (0.922)
  Pallas kernels: 42.3 us -> 38.9 us
    pallas_call x1, Pallas kernels: 39.8 us -> 37.5 us  [shards(): pl.pallas_call(fused, out_shape=jax.ShapeDtypeStruct((2, N_GZ, BLOCKS, 12...]
    pallas_call x1, Pallas kernels: 2.44 us -> 1.48 us  [shards(): pl.pallas_call(assemble, out_shape=jax.ShapeDtypeStruct((NSH, N_GZ * ROWS...]
where the time goes in v3:
time: 39.1 us; the launch traced here: 38.9 us
  Pallas kernels  38.9 us (99%)
    pallas_call x1, Pallas kernels, shards(): pl.pallas_call(fused, out_shape=jax.ShapeDtypeStruct((2, N_GZ, BLOCKS, 12...  37.5 us
    pallas_call x1, Pallas kernels, shards(): pl.pallas_call(assemble, out_shape=jax.ShapeDtypeStruct((NSH, N_GZ * ROWS...  1.48 us

profile of v3, /device:TPU:1, one launch (start us, length us, event | category | flops | bytes accessed | tf_op | source)
XLA Modules:
  0.0 38.9 jit_solution(11966816447455662208)
XLA Ops:
  0.0 37.5 %fused.1 = f32[2,4,72,128]{3,2,1,0:T(8,128)S(1)} custom-call(s32[1,32]{1,0:T(1,128)} %bitcast.9, s32[4,32]{1,0:T(4,128)} %bitcast.8, s32[1,32]{1,0:T(1,128)} %bitcast.10, bf16[12,16,3072]{2,1,0:T(8,128)(2,1)} %bitcast.7, bf16[32,256,256]{2,1,0:T(8,128)(2,1)} %eri_hbm.1), custom_call_target="tpu_custom_call" | custom-call | tf_op jit(solution)/shard_map/fused/pallas_call | solution.py:250
  37.5 1.5 %assemble.1 = f32[192,384]{1,0:T(8,128)} custom-call(f32[576,128]{1,0:T(8,128)S(1)} %bitcast.6), custom_call_target="tpu_custom_call" | custom-call | tf_op jit(solution)/shard_map/assemble/pallas_call | solution.py:279

commit v4 on v3

v4 whole, which is shorter than its diff:
```python
import jax
import jax.numpy as jnp
from jax import lax
from jax.experimental import pallas as pl
from jax.experimental.pallas import tpu as pltpu
from jax.sharding import PartitionSpec as P

SHELL = 16
PAIR = 256
TILES_DEV = 32
NSH = 192
N_GX = 8
N_Z = 8
N_GZ = 4
CAP = 8
ROWSH = 6
COLSH = 12
BLOCKS = ROWSH * COLSH
SLOTS = N_GX * CAP
CHUNKS = 2
DCHUNKS = 24
MESH = pl.DeviceIdType.MESH
F32 = jnp.float32
BF16 = jnp.bfloat16
I32 = jnp.int32


def order(rel):
    return max(0, min(2 * rel - 1, 2 * (N_GX - rel)))


def iota(shape, dim):
    return lax.broadcasted_iota(I32, shape, dim)


def fused(own_h, quart_h, sig_h, dens_hbm, eri_hbm, out_ref, own_s, quart_s, sig_s, isem, dens, eri, picked, vals, codes_out, held, ycode, zcode, mine, hots, half,
          dsem, esem, ysend, yrecv, ycsend, ycrecv, zcsend, zcrecv, rsend, rrecv, xsend, xrecv):
    gx, gy, gz = lax.axis_index("gx"), lax.axis_index("gy"), lax.axis_index("gz")
    z, core = gy // 2, lax.rem(gy, 2)

    def along_x(d, c):
        return {"gx": lax.rem(gx + N_GX - d, N_GX), "gy": z * 2 + c}

    def along_z(d):
        return {"gy": lax.rem(z + d + N_Z, N_Z) * 2 + core}

    def along_gz(d, c):
        return {"gy": z * 2 + c, "gz": lax.rem(gz + d + N_GZ, N_GZ)}

    mate = 1 - core
    step = 1 - 2 * core
    partner = {"gy": z * 2 + mate}
    ints = []
    for i, (src, dst) in enumerate(((own_h, own_s), (quart_h, quart_s), (sig_h, sig_s))):
        ints.append(pltpu.make_async_copy(src, dst, isem.at[i]))
        ints[-1].start()
    loads = []
    for c in range(DCHUNKS):
        loads.append(pltpu.make_async_copy(dens_hbm.at[:, :, pl.ds(c * 128, 128)], dens.at[pl.ds(c * COLSH, COLSH)], dsem.at[c]))
        loads[-1].start()
    per = TILES_DEV // CHUNKS
    copies = []
    for c in range(CHUNKS):
        part = pl.ds(c * per, per)
        copies.append(pltpu.make_async_copy(eri_hbm.at[part], eri.at[part], esem.at[c]))
        copies[-1].start()
    barrier = pltpu.get_barrier_semaphore()
    peers = [along_x(d, c) for d in range(1, N_GX) for c in range(2)] + [along_z(d) for d in range(1, N_Z)]
    peers += [along_gz(d, c) for d in (1, 2, 3) for c in range(2)] + [partner]
    for peer in peers:
        pl.semaphore_signal(barrier, inc=1, device_id=peer, device_id_type=MESH)

    rows = TILES_DEV * SHELL
    lane = iota((1, 128), 1)
    tile = iota((1, rows), 1) >> 4
    codes = jnp.zeros((1, 128), I32)
    spread = jnp.zeros((1, rows), I32)
    counts = jnp.int32(0)
    places = []
    for c in ints:
        c.wait()
    for t in range(TILES_DEV):
        rel = (gx - own_s[0, t] + N_GX) & (N_GX - 1)
        row = jnp.maximum(0, jnp.minimum(2 * rel - 1, 2 * (N_GX - rel)))
        seen = (counts >> (row * 4)) & 15
        counts = counts + (jnp.int32(1) << (row * 4))
        slot = row * CAP + seen
        places.append(slot)
        codes = jnp.where(lane == row * 2 * CAP + core * CAP + seen, quart_s[0, t] * NSH + quart_s[1, t], codes)
        spread = jnp.where(tile == t, slot, spread)
    for i in range(N_GX):
        codes_out[i] = jnp.where((lane >> 4) == i, codes, 0)
    gather = (iota((128, rows), 0) == spread).astype(F32).astype(BF16)
    fold = ((iota((128, PAIR), 0) & 15) == (iota((128, PAIR), 1) & 15)).astype(F32).astype(BF16)
    for load in loads:
        load.wait()
    group = iota((SHELL, 128), 1) >> 4
    for t in range(TILES_DEV):
        shell = quart_s[3, t]
        block = dens[(shell >> 3) * COLSH + quart_s[2, t]].astype(F32)
        wanted = jnp.where(sig_s[0, t] != 0, shell & 7, -1)
        picked[t * SHELL:(t + 1) * SHELL, :] = jnp.where(group == wanted, block, 0.0)
    wide = jnp.dot(picked[...].astype(BF16), fold, preferred_element_type=F32)
    wide = jnp.where((iota((rows, PAIR), 0) & 15) == (iota((rows, PAIR), 1) >> 4), wide, 0.0).astype(BF16)
    flat = jnp.dot(gather, wide, preferred_element_type=F32)
    weights = flat[:SLOTS].astype(BF16)
    terms = jnp.zeros((SLOTS, PAIR), F32)
    slots = iota((SLOTS, PAIR), 0)
    group = 4
    for t in range(0, TILES_DEV, group):
        if t % per == 0:
            copies[t // per].wait()
        many = lax.dot_general(weights, eri[t:t + group].reshape(group * PAIR, PAIR), (((1,), (1,)), ((), ())), preferred_element_type=F32)
        for i in range(group):
            terms = jnp.where(slots == places[t + i], many[:, i * PAIR:(i + 1) * PAIR], terms)
    vals[0] = terms[:, :128]
    vals[1] = terms[:, 128:]
    held[0, pl.ds(pl.multiple_of(core * CAP, CAP), CAP), :] = jnp.where(core == 0, terms[:CAP, :128], terms[:CAP, 128:])

    pl.semaphore_wait(barrier, len(peers))

    def link(src, dst, s, r, peer):
        return pltpu.make_async_remote_copy(src_ref=src, dst_ref=dst, send_sem=s, recv_sem=r, device_id=peer, device_id_type=MESH)

    def send(src, dst, s, r, peer):
        copy = link(src, dst, s, r, peer)
        copy.start()
        started.append(copy)
        return copy

    started = []
    near = [1, 7, 2]
    far = [6, 3, 5, 4]

    def value_rows(r, c):
        return held.at[0, pl.ds(pl.multiple_of(r * 2 * CAP + c * CAP, CAP), CAP)]

    def give(r, c, peer):
        send(codes_out.at[r], ycode.at[r * 2 + core], ycsend.at[r * 2 + c], ycrecv.at[r * 2 + core], peer)
        send(vals.at[c, pl.ds(r * CAP, CAP)], value_rows(r, core), ysend.at[r * 2 + c], yrecv.at[r * 2 + core], peer)

    for d in far[::-1] + near[::-1]:
        for c in range(2):
            give(order(d), c, along_x(d, c))
    give(0, mate, partner)

    def value_in(r, c):
        link(vals.at[0, pl.ds(0, CAP)], value_rows(r, c), ysend.at[0], yrecv.at[r * 2 + c], partner).wait_recv()

    def code_in(r, c):
        link(codes_out.at[0], ycode.at[r * 2 + c], ycsend.at[0], ycrecv.at[r * 2 + c], partner).wait_recv()

    firsts, sizes = (0, 64), (64, 64)

    def hop(src, distance, dst, g):
        part = pl.ds(firsts[g], sizes[g])
        i = dst * 2 + g
        inward[dst, g] = send(held.at[src, part], held.at[dst, part], rsend.at[i], rrecv.at[i], along_z(distance))

    inward = {}
    rows = iota((2 * BLOCKS, 128), 0)
    other = (rows >= BLOCKS).astype(I32)
    inner = rows - other * BLOCKS
    bra = jnp.zeros_like(inner)
    for i in range(1, ROWSH):
        bra = bra + (inner >= i * COLSH).astype(I32)
    ket = inner - bra * COLSH
    column = jnp.where(other == 1, (z * 2 + 1 - core) * COLSH, gy * COLSH)
    wanted = bra * NSH + column + ket

    value_in(0, mate)
    for g, ds in enumerate(((1, 7, 2), (6, 3, 5, 4))):
        for d in ds:
            for c in range(2):
                value_in(order(d), c)
        hop(0, 2, 3, g)
        hop(0, -2, 4, g)
        hop(0, 1, 1, g)
        hop(0, -1, 2, g)
    code_in(0, mate)
    total = codes_out[0] + ycode[mate]
    for r in range(1, N_GX):
        for c in range(2):
            code_in(r, c)
            total = total + ycode[r * 2 + c]
    mine[...] = total
    zcode[0] = total
    zcode_in = []
    for d, slot in ((4, 7), (3, 5), (5, 6), (2, 3), (6, 4), (1, 1), (7, 2)):
        zcode_in.append(send(mine, zcode.at[slot], zcsend.at[slot], zcrecv.at[slot], along_z(d)))

    for g in range(2):
        inward[3, g].wait_recv()
        if g in (0,):
            hop(3, 2, 7, g)
        hop(3, 1, 5, g)
        inward[4, g].wait_recv()
        if g not in (0,):
            hop(4, -2, 7, g)
        hop(4, -1, 6, g)

    for c in zcode_in:
        c.wait_recv()
    for i in range(N_Z):
        hot = (wanted == zcode[i]).astype(F32).astype(BF16)
        hots[i, :, 0:128] = hot
        hots[i, :, 128:256] = hot

    acc = jnp.zeros((2 * BLOCKS, 128), F32)
    for i in (0, 3, 4, 1, 2, 5, 6, 7):
        if i not in (0, 3, 4):
            for g in range(2):
                inward[i, g].wait_recv()
        top = held[i].astype(BF16)
        low = (held[i] - top.astype(F32)).astype(BF16)
        acc = acc + jnp.dot(hots[i], jnp.concatenate([top, low], axis=0), preferred_element_type=F32)
    half[...] = acc[BLOCKS:]
    out_ref[core, gz] = acc[:BLOCKS]

    home = out_ref.at[core, gz]

    def spread_out(i, src, peer):
        return send(src, home, xsend.at[i], xrecv.at[i], peer)

    last = [
        spread_out(6, half, partner),
        spread_out(4, home, along_gz(2, core)),
        spread_out(5, half, along_gz(2, mate)),
        spread_out(0, home, along_gz(step, core)),
        spread_out(1, half, along_gz(-step, mate)),
        spread_out(2, home, along_gz(-step, core)),
        spread_out(3, half, along_gz(step, mate)),
    ]
    for c in last:
        c.wait_recv()
    for c in started:
        c.wait_send()


def assemble(got_ref, out_ref, wide):
    group = iota((4 * ROWSH, 128), 1) >> 4
    pieces = [[got_ref[pl.ds(h * N_GZ * BLOCKS + k, 4 * ROWSH, stride=COLSH), :] for h in range(2)] for k in range(COLSH)]
    for a in range(SHELL):
        for j, ks in enumerate((range(8), range(8, COLSH))):
            line = jnp.zeros((4 * ROWSH, 128), F32)
            for k in ks:
                shift = ((k - a) % 8) * 16
                src = pieces[k][a // 8]
                moved = pltpu.roll(src, shift, 1) if shift else src
                line = jnp.where(group == k % 8, moved, line)
            wide[j, pl.ds(a, 4 * ROWSH, stride=SHELL), :] = line
    out_ref[:128, :] = wide[0].T
    out_ref[128:, :] = wide[1].T[:NSH - 128, :]


def shards(eri, owner, quartet, significance, density):
    hbm = pl.BlockSpec(memory_space=pltpu.HBM)
    vmem = pl.BlockSpec(memory_space=pltpu.VMEM)
    dma = pltpu.SemaphoreType.DMA
    operands = (owner.T, quartet.T, significance[None, :], density.reshape(COLSH, SHELL, density.shape[1]), eri)
    got = pl.pallas_call(
        fused,
        out_shape=jax.ShapeDtypeStruct((2, N_GZ, BLOCKS, 128), F32),
        in_specs=[hbm] * 5,
        out_specs=vmem,
        scratch_shapes=[
            pltpu.SMEM((1, TILES_DEV), I32),
            pltpu.SMEM((4, TILES_DEV), I32),
            pltpu.SMEM((1, TILES_DEV), I32),
            dma((3,)),
            pltpu.VMEM((DCHUNKS * COLSH, SHELL, 128), BF16),
            pltpu.VMEM(eri.shape, BF16),
            pltpu.VMEM((TILES_DEV * SHELL, 128), F32),
            pltpu.VMEM((2, SLOTS, 128), F32),
            pltpu.VMEM((N_GX, 1, 128), I32),
            pltpu.VMEM((N_Z, 2 * SLOTS, 128), F32),
            pltpu.VMEM((2 * N_GX, 1, 128), I32),
            pltpu.VMEM((N_Z, 1, 128), I32),
            pltpu.VMEM((1, 128), I32),
            pltpu.VMEM((N_Z, 2 * BLOCKS, PAIR), BF16),
            pltpu.VMEM((BLOCKS, 128), F32),
            dma((DCHUNKS,)), dma((CHUNKS,)),
            dma((16,)), dma((16,)), dma((16,)), dma((16,)), dma((N_Z,)), dma((N_Z,)),
            dma((16,)), dma((16,)), dma((7,)), dma((7,)),
        ],
        compiler_params=pltpu.CompilerParams(collective_id=0, has_side_effects=True, vmem_limit_bytes=16000000),
        name="fused",
    )(*[pltpu.with_memory_space_constraint(a, pltpu.HBM) for a in operands])
    turned = pl.pallas_call(
        assemble,
        out_shape=jax.ShapeDtypeStruct((NSH, N_GZ * ROWSH * SHELL), F32),
        in_specs=[vmem],
        out_specs=vmem,
        scratch_shapes=[pltpu.VMEM((2, N_GZ * ROWSH * SHELL, 128), F32)],
        compiler_params=pltpu.CompilerParams(vmem_limit_bytes=16000000),
        name="assemble",
    )(got.reshape(2 * N_GZ * BLOCKS, 128))
    return turned.T


def solution(mesh):
    in_specs = (
        P(("gx", "gy", "gz"), None, None),
        P(("gx", "gy", "gz"), None),
        P(("gx", "gy", "gz"), None),
        P(("gx", "gy", "gz")),
        P("gy", None),
    )
    return jax.shard_map(shards, mesh=mesh, in_specs=in_specs, out_specs=P("gx", "gy"), check_vma=False)
```

time: 39.1 us -> 38.1 us (0.974)
  Pallas kernels: 38.9 us -> 38 us
    pallas_call x1, Pallas kernels: 37.5 us -> 36.5 us  [shards(): pl.pallas_call(fused, out_shape=jax.ShapeDtypeStruct((2, N_GZ, BLOCKS, 12...]
where the time goes in v4:
time: 38.1 us; the launch traced here: 38 us
  Pallas kernels  38 us (100%)
    pallas_call x1, Pallas kernels, shards(): pl.pallas_call(fused, out_shape=jax.ShapeDtypeStruct((2, N_GZ, BLOCKS, 12...  36.5 us
    pallas_call x1, Pallas kernels, shards(): pl.pallas_call(assemble, out_shape=jax.ShapeDtypeStruct((NSH, N_GZ * ROWS...  1.48 us

profile of v4, /device:TPU:1, one launch (start us, length us, event | category | flops | bytes accessed | tf_op | source)
XLA Modules:
  0.0 38.0 jit_solution(10402326011752486947)
XLA Ops:
  0.0 36.5 %fused.1 = f32[2,4,72,128]{3,2,1,0:T(8,128)S(1)} custom-call(s32[1,32]{1,0:T(1,128)} %bitcast.9, s32[4,32]{1,0:T(4,128)} %bitcast.8, s32[1,32]{1,0:T(1,128)} %bitcast.10, bf16[12,16,3072]{2,1,0:T(8,128)(2,1)} %bitcast.7, bf16[32,256,256]{2,1,0:T(8,128)(2,1)} %eri_hbm.1), custom_call_target="tpu_custom_call" | custom-call | tf_op jit(solution)/shard_map/fused/pallas_call | solution.py:261
  36.5 1.5 %assemble.1 = f32[192,384]{1,0:T(8,128)} custom-call(f32[576,128]{1,0:T(8,128)S(1)} %bitcast.6), custom_call_target="tpu_custom_call" | custom-call | tf_op jit(solution)/shard_map/assemble/pallas_call | solution.py:289

commit v5 on v4

--- a/solution.py
+++ b/solution.py
@@ -67,7 +67,7 @@
     barrier = pltpu.get_barrier_semaphore()
     peers = [along_x(d, c) for d in range(1, N_GX) for c in range(2)] + [along_z(d) for d in range(1, N_Z)]
     peers += [along_gz(d, c) for d in (1, 2, 3) for c in range(2)] + [partner]
-    for peer in peers:
+    for peer in peers[::-1]:
         pl.semaphore_signal(barrier, inc=1, device_id=peer, device_id_type=MESH)
 
     rows = TILES_DEV * SHELL
@@ -201,19 +201,27 @@
 
     for c in zcode_in:
         c.wait_recv()
-    for i in range(N_Z):
+    early, late = (0, 3, 4, 1, 2), (5, 6, 7)
+    for n, i in enumerate(early + late):
         hot = (wanted == zcode[i]).astype(F32).astype(BF16)
-        hots[i, :, 0:128] = hot
-        hots[i, :, 128:256] = hot
-
-    acc = jnp.zeros((2 * BLOCKS, 128), F32)
-    for i in (0, 3, 4, 1, 2, 5, 6, 7):
-        if i not in (0, 3, 4):
-            for g in range(2):
-                inward[i, g].wait_recv()
-        top = held[i].astype(BF16)
-        low = (held[i] - top.astype(F32)).astype(BF16)
-        acc = acc + jnp.dot(hots[i], jnp.concatenate([top, low], axis=0), preferred_element_type=F32)
+        hots[:, n * 256:n * 256 + 128] = hot
+        hots[:, n * 256 + 128:n * 256 + 256] = hot
+
+    def place(blocks, first):
+        parts = []
+        for i in blocks:
+            top = held[i].astype(BF16)
+            parts += [top, (held[i] - top.astype(F32)).astype(BF16)]
+        return jnp.dot(hots[:, first * 256:(first + len(blocks)) * 256], jnp.concatenate(parts, axis=0), preferred_element_type=F32)
+
+    for i in (1, 2):
+        for g in range(2):
+            inward[i, g].wait_recv()
+    acc = place(early, 0)
+    for i in late:
+        for g in range(2):
+            inward[i, g].wait_recv()
+    acc = acc + place(late, len(early))
     half[...] = acc[BLOCKS:]
     out_ref[core, gz] = acc[:BLOCKS]
 
@@ -277,7 +285,7 @@
             pltpu.VMEM((2 * N_GX, 1, 128), I32),
             pltpu.VMEM((N_Z, 1, 128), I32),
             pltpu.VMEM((1, 128), I32),
-            pltpu.VMEM((N_Z, 2 * BLOCKS, PAIR), BF16),
+            pltpu.VMEM((2 * BLOCKS, N_Z * PAIR), BF16),
             pltpu.VMEM((BLOCKS, 128), F32),
             dma((DCHUNKS,)), dma((CHUNKS,)),
             dma((16,)), dma((16,)), dma((16,)), dma((16,)), dma((N_Z,)), dma((N_Z,)),

time: 38.1 us -> 37.9 us (level)
  no operation moved by 1% of the time
where the time goes in v5:
time: 37.9 us; the launch traced here: 37.8 us
  Pallas kernels  37.8 us (100%)
    pallas_call x1, Pallas kernels, shards(): pl.pallas_call(fused, out_shape=jax.ShapeDtypeStruct((2, N_GZ, BLOCKS, 12...  36.3 us
    pallas_call x1, Pallas kernels, shards(): pl.pallas_call(assemble, out_shape=jax.ShapeDtypeStruct((NSH, N_GZ * ROWS...  1.48 us

profile of v5, /device:TPU:1, one launch (start us, length us, event | category | flops | bytes accessed | tf_op | source)
XLA Modules:
  0.0 37.8 jit_solution(15239431843565494340)
XLA Ops:
  0.0 36.3 %fused.1 = f32[2,4,72,128]{3,2,1,0:T(8,128)S(1)} custom-call(s32[1,32]{1,0:T(1,128)} %bitcast.9, s32[4,32]{1,0:T(4,128)} %bitcast.8, s32[1,32]{1,0:T(1,128)} %bitcast.10, bf16[12,16,3072]{2,1,0:T(8,128)(2,1)} %bitcast.7, bf16[32,256,256]{2,1,0:T(8,128)(2,1)} %eri_hbm.1), custom_call_target="tpu_custom_call" | custom-call | tf_op jit(solution)/shard_map/fused/pallas_call | solution.py:269
  36.3 1.5 %assemble.1 = f32[192,384]{1,0:T(8,128)} custom-call(f32[576,128]{1,0:T(8,128)S(1)} %bitcast.6), custom_call_target="tpu_custom_call" | custom-call | tf_op jit(solution)/shard_map/assemble/pallas_call | solution.py:297

commit v6 on v5

--- a/solution.py
+++ b/solution.py
@@ -218,26 +218,28 @@
         for g in range(2):
             inward[i, g].wait_recv()
     acc = place(early, 0)
-    for i in late:
-        for g in range(2):
-            inward[i, g].wait_recv()
-    acc = acc + place(late, len(early))
+    for n, blocks in ((5, (5, 6)), (7, (7,))):
+        for i in blocks:
+            for g in range(2):
+                inward[i, g].wait_recv()
+        acc = acc + place(blocks, n)
     half[...] = acc[BLOCKS:]
-    out_ref[core, gz] = acc[:BLOCKS]
-
     home = out_ref.at[core, gz]
 
     def spread_out(i, src, peer):
         return send(src, home, xsend.at[i], xrecv.at[i], peer)
 
     last = [
+        spread_out(5, half, along_gz(2, mate)),
         spread_out(6, half, partner),
+        spread_out(1, half, along_gz(-step, mate)),
+        spread_out(3, half, along_gz(step, mate)),
+    ]
+    out_ref[core, gz] = acc[:BLOCKS]
+    last += [
         spread_out(4, home, along_gz(2, core)),
-        spread_out(5, half, along_gz(2, mate)),
         spread_out(0, home, along_gz(step, core)),
-        spread_out(1, half, along_gz(-step, mate)),
         spread_out(2, home, along_gz(-step, core)),
-        spread_out(3, half, along_gz(step, mate)),
     ]
     for c in last:
         c.wait_recv()

time: 37.9 us -> 37.7 us (level); the launches traced: 37.8 us -> 37.2 us
  Pallas kernels: 37.8 us -> 37.1 us
    pallas_call x1, Pallas kernels: 36.3 us -> 35.7 us  [shards(): pl.pallas_call(fused, out_shape=jax.ShapeDtypeStruct((2, N_GZ, BLOCKS, 12...]
where the time goes in v6:
time: 37.7 us; the launch traced here: 37.2 us
  Pallas kernels  37.1 us (98%)
    pallas_call x1, Pallas kernels, shards(): pl.pallas_call(fused, out_shape=jax.ShapeDtypeStruct((2, N_GZ, BLOCKS, 12...  35.7 us
    pallas_call x1, Pallas kernels, shards(): pl.pallas_call(assemble, out_shape=jax.ShapeDtypeStruct((NSH, N_GZ * ROWS...  1.48 us

profile of v6, /device:TPU:1, one launch (start us, length us, event | category | flops | bytes accessed | tf_op | source)
XLA Modules:
  0.0 37.2 jit_solution(6032644610981887507)
XLA Ops:
  0.0 35.7 %fused.1 = f32[2,4,72,128]{3,2,1,0:T(8,128)S(1)} custom-call(s32[1,32]{1,0:T(1,128)} %bitcast.9, s32[4,32]{1,0:T(4,128)} %bitcast.8, s32[1,32]{1,0:T(1,128)} %bitcast.10, bf16[12,16,3072]{2,1,0:T(8,128)(2,1)} %bitcast.7, bf16[32,256,256]{2,1,0:T(8,128)(2,1)} %eri_hbm.1), custom_call_target="tpu_custom_call" | custom-call | tf_op jit(solution)/shard_map/fused/pallas_call | solution.py:271
  35.7 1.5 %assemble.1 = f32[192,384]{1,0:T(8,128)} custom-call(f32[576,128]{1,0:T(8,128)S(1)} %bitcast.6), custom_call_target="tpu_custom_call" | custom-call | tf_op jit(solution)/shard_map/assemble/pallas_call | solution.py:299
